TPU v7x, 128 devices: a whole 4x4x4 slice. The times are simulated.
128 devices in a mesh: row: 16 (over z, y), col: 8 (over x, core).
Axes of the slice: x: 4, y: 4, z: 4, core: 2. Of those that a mesh axis runs over, the one named last changes fastest.
Arguments:
- act_quant: bfloat16 [1024, 8192], P('row', 'col'), may hold values from -127 to 127, as said below
- act_scale: float32 [1024], replicated, may hold values from 0.004 to 0.04
- gate_up_quant: bfloat16 [2, 8192, 29568], P(None, 'col', 'row'), may hold values from -127 to 127, as said below
- gate_up_scale: float32 [2, 29568], P(None, 'row'), may hold values from 5e-05 to 0.0005
- down_quant: bfloat16 [29568, 8192], P('row', 'col'), may hold values from -127 to 127, as said below
- down_scale: float32 [8192], P('col'), may hold values from 3e-05 to 0.0003
Outputs:
- mixed_out: bfloat16 [1024, 8192], P('row', 'col')
Inputs may be any that keep to these rules, and one draw needn't show every extreme that they name: `act_quant`: whole numbers. `gate_up_quant`: whole numbers. `down_quant`: whole numbers.
All inputs are finite; a program needn't handle non-finite values.
Results may differ from a plain program's by a relative error of at most 0.005.
Values may be sent and summed in bfloat16 or wider, within the bound.
A program may use at most 128 MiB of HBM per device.

v0:
```python
import jax
import jax.numpy as jnp
from jax import lax
from jax.sharding import PartitionSpec as P


def laid_out(tiles, dim):
    dims = list(tiles.shape[1:])
    dims[dim] *= tiles.shape[0]
    return jnp.moveaxis(tiles, 0, dim).reshape(dims)


def copy_for_each(shard, axis):
    copies = jnp.broadcast_to(shard, (lax.axis_size(axis), *shard.shape))
    return lax.all_to_all(copies, axis, split_axis=0, concat_axis=0, tiled=True)


def gather_directly(shard, axis, dim):
    return laid_out(copy_for_each(shard, axis), dim)


def in_blocks(shard, dim, count):
    dims = shard.shape
    tiles = shard.reshape(*dims[:dim], count, dims[dim] // count, *dims[dim + 1 :])
    return jnp.moveaxis(tiles, dim, 0)


def sent_and_summed(shard, axis, dim):
    tiles = in_blocks(shard, dim, lax.axis_size(axis))
    arrived = lax.all_to_all(tiles, axis, split_axis=0, concat_axis=0, tiled=True)
    return arrived.sum(axis=0)


def body(act_quant, act_scale, gate_up_quant, gate_up_scale, down_quant, down_scale):
    feature_width = gate_up_quant.shape[2]
    gathered = gather_directly(act_quant, "row", 0)
    share_rows = gathered.shape[0] // lax.axis_size("col")
    gate_part = jnp.dot(gathered, gate_up_quant[0], preferred_element_type=jnp.float32)
    up_part = jnp.dot(gathered, gate_up_quant[1], preferred_element_type=jnp.float32)
    summed = lax.psum_scatter(
        jnp.concatenate([gate_part, up_part], axis=1), "col", scatter_dimension=0, tiled=True
    )
    token_scale = lax.dynamic_slice_in_dim(
        act_scale, lax.axis_index("col") * share_rows, share_rows, 0
    )
    gate_val = summed[:, :feature_width] * token_scale[:, None] * gate_up_scale[0][None, :]
    up_val = summed[:, feature_width:] * token_scale[:, None] * gate_up_scale[1][None, :]
    hidden = (jax.nn.silu(gate_val) * up_val).astype(jnp.bfloat16)
    hidden = lax.all_gather(hidden, "col", axis=0, tiled=True)
    mixed_out = sent_and_summed(
        jnp.dot(hidden, down_quant, preferred_element_type=jnp.float32) * down_scale[None, :],
        "row",
        0,
    )
    return mixed_out.astype(jnp.bfloat16)


def solution(mesh):
    in_specs = (
        P("row", "col"),
        P(),
        P(None, "col", "row"),
        P(None, "row"),
        P("row", "col"),
        P("col"),
    )
    out_specs = P("row", "col")
    return jax.shard_map(body, mesh=mesh, in_specs=in_specs, out_specs=out_specs, check_vma=False)
```

profile of v0, /device:TPU:0, one launch (start us, length us, event | category | flops | bytes accessed | tf_op | source)
XLA Modules:
  0.0 256.0 jit_solution(661841467545645263)
XLA Ops:
  6.5 0.0 reduce-scatter.2.cloned.1.call-start
  6.5 1.2 broadcast_in_dim.2
  7.7 0.0 slice-start
  7.7 36.6 %all_to_all.10 = bf16[16,64,1024]{2,1,0:T(8,128)(2,1)S(1)} all-to-all(bf16[16,64,1024]{2,1,0:T(8,128)(2,1)S(1)} %broadcast_in_dim.2), channel_id=1, replica_groups=mesh['row'=16,'col'=8] {'row'}, dimensions={0} | all-to-all | bytes 4194304 | tf_op jit(solution)/shard_map/all_to_all | solution.py:15
  44.3 0.0 slice-start.1
  44.3 6.5 %fusion = f32[1024,1848]{0,1:T(8,128)S(1)} fusion(bf16[1024,1024]{1,0:T(8,128)(2,1)S(1)} %bitcast.13, bf16[2,1024,1848]{1,2,0:T(8,128)(2,1)} %param.8), kind=kOutput, calls=%fused_computation.1 | convolution fusion | flops 3875536896 | bytes 13451264 | tf_op jit(solution)/shard_map/dot_general | solution.py:39
  50.9 0.0 slice-done
  50.9 0.0 slice-done.1
  50.9 4.2 %fusion.2 = f32[1024,1848]{0,1:T(8,128)S(1)} fusion(bf16[1024,1024]{1,0:T(8,128)(2,1)S(1)} %bitcast.14, bf16[2,1024,1848]{1,2,0:T(8,128)(2,1)S(1)} %bitcast.16), kind=kOutput, calls=%fused_computation.3 | convolution fusion | flops 3875536896 | bytes 13451264 | tf_op jit(solution)/shard_map/dot_general | solution.py:38
  55.1 6.0 %pad_maximum_fusion = f32[1024,3696]{0,1:T(8,128)} fusion(f32[1024,1848]{0,1:T(8,128)S(1)} %fusion, f32[1024,1848]{0,1:T(8,128)S(1)} %fusion.2), kind=kLoop, calls=%fused_computation | loop fusion | flops 3784704 | bytes 30277632 | tf_op jit(solution)/shard_map/concatenate | solution.py:41
  61.1 0.0 copy-start
  61.1 0.0 copy-start.1
  61.1 0.0 reduce-scatter.2.cloned.1.call-update
  61.1 0.2 all-gather.2.cloned.1.call-start
  61.4 0.8 dynamic_slice.3
  62.1 0.0 copy-done
  62.2 81.1 %reduce-scatter.2.cloned.1.call-done = f32[128,3696]{0,1:T(8,128)} async-done(((f32[1024,3696]{0,1:T(8,128)}), f32[128,3696]{0,1:T(8,128)}) %reduce-scatter.2.cloned.1.call-update) | async-done | bytes 1892368 | tf_op jit(solution)/shard_map/reduce_scatter | solution.py:40
  143.3 3.0 %fusion.8 = bf16[128,1848]{0,1:T(8,128)(2,1)} fusion(f32[128,3696]{0,1:T(8,128)} %reduce-scatter.2.cloned.1.call-done, f32[1848]{0:T(1024)S(1)} %get-tuple-element.6, f32[1848]{0:T(1024)S(1)} %get-tuple-element.5, f32[128]{0:T(128)S(1)} %dynamic_slice.3), kind=kLoop, calls=%fused_computation.11 | loop fusion | flops 2365440 | bytes 2380736 | tf_op jit(solution)/shard_map/convert_element_type | solution.py:48
  146.3 0.0 all-gather.2.cloned.1.call-update
  146.3 33.6 %all-gather.2.cloned.1.call-done = bf16[1024,1848]{0,1:T(8,128)(2,1)} async-done(((bf16[128,1848]{0,1:T(8,128)(2,1)}), bf16[1024,1848]{0,1:T(8,128)(2,1)}) %all-gather.2.cloned.1.call-update) | async-done | bytes 3784720 | tf_op jit(solution)/shard_map/all_gather | solution.py:49
  179.9 0.0 copy-done.1
  179.9 8.0 %convolution_multiply_fusion = f32[1024,1024]{1,0:T(8,128)S(1)} fusion(bf16[1024,1848]{0,1:T(8,128)(2,1)} %all-gather.2.cloned.1.call-done, bf16[1848,1024]{1,0:T(8,128)(2,1)} %param.10, f32[1024]{0:T(1024)S(1)} %copy-done.1), kind=kOutput, calls=%fused_computation.7 | convolution fusion | flops 3876585472 | bytes 11767808 | tf_op jit(solution)/shard_map/dot_general | solution.py:51
  187.8 58.2 %all_to_all.11 = f32[16,64,1024]{2,1,0:T(8,128)} all-to-all(f32[16,64,1024]{2,1,0:T(8,128)S(1)} %bitcast.12), channel_id=1, replica_groups=mesh['row'=16,'col'=8] {'row'}, dimensions={0} | all-to-all | bytes 8388608 | tf_op jit(solution)/shard_map/all_to_all | solution.py:30
  246.0 3.2 %reduce_sum.9 = bf16[64,1024]{1,0:T(8,128)(2,1)} reduce(f32[16,64,1024]{2,1,0:T(8,128)} %all_to_all.11, f32[]{:T(128)} %constant.14.clone.1), dimensions={0}, to_apply=%region_1.2 | reduce | flops 983040 | bytes 4325380 | tf_op jit(solution)/shard_map/reduce_sum | solution.py:31
  (2 shorter events, 0.0 us)
Async XLA Ops:
  6.5 136.7 %reduce-scatter.2.cloned.1.call-start = ((), (), s32[]{:S(2)}) async-start(), calls=%async_computation.3 | async-start | bytes 17031168 | tf_op jit(solution)/shard_map/reduce_scatter | solution.py:40
  7.7 43.2 %slice-start = ((s8[7569408]{0:T(1024)(128)(4,1)}), s8[4194304]{0:T(1024)(128)(4,1)S(1)}, s32[]{:S(2)}) async-start(s8[7569408]{0:T(1024)(128)(4,1)} %bitcast.15), calls=%async_computation.5 | async-start | bytes 8388608
  44.3 6.5 %slice-start.1 = ((s8[7569408]{0:T(1024)(128)(4,1)}), s8[3375104]{0:T(1024)(128)(4,1)S(1)}, s32[]{:S(2)}) async-start(s8[7569408]{0:T(1024)(128)(4,1)} %bitcast.15), calls=%async_computation.6 | async-start | bytes 6750208
  61.1 1.0 copy-start
  61.1 118.8 %copy-start.1 = (f32[1024]{0:T(1024)S(1)}, f32[1024]{0:T(1024)}, u32[]{:S(2)}) copy-start(f32[1024]{0:T(1024)} %param.11) | copy-start | bytes 12292
  61.1 118.7 %all-gather.2.cloned.1.call-start = ((), (), s32[]{:S(2)}) async-start(), calls=%async_computation.4 | async-start | bytes 4257792 | tf_op jit(solution)/shard_map/all_gather | solution.py:49
Sparse Core Ops, SparseCore 0:
  61.2 81.9 reduce-scatter.1
  146.4 33.3 all-gather.1
where the time goes:
time: 256 us
  waiting for transfers between devices  115 us (45%)
  blocking collectives  94.8 us (37%)
  matrix products  18.7 us (7%)
  between operations  13.5 us (5%)
  other arithmetic  12.1 us (5%)
    reduce_scatter x1, waiting for transfers between devices, body(): lax.psum_scatter(jnp.concatenate([gate_part, up_part], axis=1), 'col', sc...  81.1 us
    all_to_all x1, blocking collectives, sent_and_summed(): lax.all_to_all(tiles, axis, split_axis=0, concat_axis=0, tiled=True)  58.2 us
    all_to_all x1, blocking collectives, copy_for_each(): return lax.all_to_all(copies, axis, split_axis=0, concat_axis=0, tiled=True)  36.6 us
    all_gather x1, waiting for transfers between devices, body(): hidden = lax.all_gather(hidden, 'col', axis=0, tiled=True)  33.6 us
    dot_general x1, matrix products, body(): jnp.dot(hidden, down_quant, preferred_element_type=jnp.float32)  7.97 us
    dot_general x1, matrix products, body(): jnp.dot(gathered, gate_up_quant[1], preferred_element_type=jnp.float32)  6.53 us
    concatenate x1, other arithmetic, body(): jnp.concatenate([gate_part, up_part], axis=1)  5.96 us
  transfers between devices with their start and end apart: 2, of which 2 were waited for; matrix products, arithmetic and copies ran while one was open for 0% of the time, Pallas kernels for 0%

commit v1 on v0

v1 whole, which is shorter than its diff:
```python
import jax
import jax.numpy as jnp
from jax import lax
from jax.experimental import pallas as pl
from jax.experimental.pallas import tpu as pltpu
from jax.sharding import PartitionSpec as P

MESH = pl.DeviceIdType.MESH
CHUNKS = 4
F32 = jnp.float32
BF16 = jnp.bfloat16
OFFSETS = [(a, b) for a in range(4) for b in range(4) if a or b]
PIECES = ((0, 1024, 0), (1024, 768, 0), (1792, 1024, 1), (2816, 880, 1))
ORDER = (
    "A00 A10 A20 A30", "B00 B10 B20 B30", "A01 A11 C00 C10", "A21 A31 C20 C30",
    "B01 B11 B21 B31", "A02 A12 A22 A32", "D.0 C01 C11", "C21 C31 B02",
    "B12 B22 B32 E.0", "A03 A13 A23 A33", "D.1 e.0 C02 C12", "C22 C32 B03",
    "B13 B23 B33 E.1", "F.0 D.2 C03 C13", "C23 C33 e.1", "E.2 F.1 J.0 D.3",
    "e.2 F.2 E.3 J.1", "e.3 F.3 J.2 J.3",
)


def kernel(
    act_hbm, act_scale, gate_up_hbm, gate_up_scale, down_hbm, down_scale, out,
    act, w, dn, acc, pair, first, direct, merge, own, first_in, left_in, right_in,
    hid, o_send, o_recv, scale, load_sem, send_sem, recv_sem,
):
    n, rows, tok, width = act.shape
    feats = hid.shape[3]
    row, col = lax.axis_index("row"), lax.axis_index("col")
    z, y, x, core = row // 4, row % 4, col // 2, col % 2
    x1, x2, x3 = (x + 1) % 4, (x + 2) % 4, (x + 3) % 4
    xp, xm = (row, x1 * 2 + core), (row, x3 * 2 + core)
    mate = (row, x * 2 + 1 - core)
    peers = [((z + a) % 4 * 4 + (y + b) % 4, col) for a, b in OFFSETS]

    def load(src, dst, index):
        copy = pltpu.make_async_copy(src, dst, load_sem.at[index])
        copy.start()
        return copy

    own_loads = [
        load(act_hbm.at[pl.ds(tok * i, tok)], act.at[i, row], i) for i in range(n)
    ]
    w_loads = [
        load(gate_up_hbm.at[pl.ds(s, m)], w.at[pl.ds(s, m)], n + p)
        for p, (s, m, _) in enumerate(PIECES)
    ]
    dn_load = load(down_hbm, dn, n + len(PIECES))

    names = {}
    copies = [{} for _ in range(n)]

    def send(i, name, src, dst, device):
        index = names.setdefault(name, len(names))
        copy = pltpu.make_async_remote_copy(
            src_ref=src, dst_ref=dst, send_sem=send_sem.at[i, index],
            recv_sem=recv_sem.at[i, index], device_id=device, device_id_type=MESH,
        )
        copy.start()
        copies[i][name] = copy

    def got(i, *which):
        for name in which:
            copies[i][name].wait_recv()

    barrier = pltpu.get_barrier_semaphore()
    near = [xp, xm, mate, *peers]
    for device in near:
        pl.semaphore_signal(barrier, inc=1, device_id=device, device_id_type=MESH)

    lane = lax.broadcasted_iota(jnp.int32, (128, 128), 1)
    line = lax.broadcasted_iota(jnp.int32, (128, 128), 0)
    mine = jnp.broadcast_to(act_scale[pl.ds(col, 1), :], (128, 128))
    column = jnp.sum(jnp.where(lane == line, mine, 0.0), axis=1, keepdims=True)
    scale[...] = jnp.broadcast_to(column, (128, 128))

    pl.semaphore_wait(barrier, len(near))

    for i in range(n):
        own_loads[i].wait()
        for q, peer in enumerate(peers):
            send(i, f"a{q}", act.at[i, row], act.at[i, row], peer)

    def stage_a(i, p):
        start, size, _ = PIECES[p]
        cols = pl.ds(start, size)
        if p == 0:
            got(i, *[f"a{q}" for q in range(len(peers))])
            if i >= 2:
                for q in range(len(PIECES)):
                    copies[i - 2].pop(f"p{q}").wait_send()
        if i == 0:
            w_loads[p].wait()
        part = lax.dot_general(
            act[i].reshape(rows * tok, width), w[cols, :], (((1,), (1,)), ((), ())),
            preferred_element_type=F32,
        )
        s = i % 2
        acc[s, :, :, :, cols] = part.reshape(4, 2, 2 * tok, size)
        send(i, f"p{p}", acc.at[s, :, 1 - core, :, cols], pair.at[i, :, :, cols], mate)

    def stage_b(i, p):
        start, size, side = PIECES[p]
        cols = pl.ds(start, size)
        s = i % 2

        def both(d):
            return acc[s, d, core, :, cols] + pair[i, d, :, cols]

        got(i, f"p{p}")
        near_dev, far_dev = (xm, xp) if side == 0 else (xp, xm)
        near_x, far_x = (x3, x1) if side == 0 else (x1, x3)
        landing = right_in if side == 0 else left_in
        first[i, :, cols] = both(x2).astype(BF16)
        send(i, f"s{p}", first.at[i, :, cols], first_in.at[i, :, cols], far_dev)
        direct[i, :, cols] = both(near_x).astype(BF16)
        send(i, f"d{p}", direct.at[i, :, cols], landing.at[i, :, cols], near_dev)
        merge[i, :, cols] = both(far_x)
        own[i, :, cols] = both(x)

    def stage_c(i, p):
        start, size, side = PIECES[p]
        cols = pl.ds(start, size)
        far_dev, landing = (xp, left_in) if side == 0 else (xm, right_in)
        got(i, f"s{p}")
        copies[i].pop(f"s{p}").wait_send()
        first[i, :, cols] = (merge[i, :, cols] + first_in[i, :, cols].astype(F32)).astype(BF16)
        send(i, f"m{p}", first.at[i, :, cols], landing.at[i, :, cols], far_dev)

    def pass_on(i, name, block, device, start=0, size=None):
        part = hid.at[i, block, pl.ds(start, size or 2 * tok)]
        send(i, name, part, part, device)

    def stage_d(i):
        got(i, *[kind + str(p) for kind in "dm" for p in range(len(PIECES))])
        total = own[i] + left_in[i].astype(F32) + right_in[i].astype(F32)
        token = jnp.concatenate(
            [scale[pl.ds(tok * i, tok), 0:1], scale[pl.ds(64 + tok * i, tok), 0:1]], axis=0
        )
        gate = total[:, :feats] * token * gate_up_scale[0:1, :]
        up = total[:, feats:] * token * gate_up_scale[1:2, :]
        hid[i, col] = (gate / (1.0 + jnp.exp(-gate)) * up).astype(BF16)
        pass_on(i, "hp", col, xp)
        pass_on(i, "hm", col, xm)
        pass_on(i, "hc", col, mate)

    def stage_e(i):
        left, right = x3 * 2 + core, x1 * 2 + core
        got(i, "hp")
        pass_on(i, "hfp", left, xp, 0, tok)
        pass_on(i, "hcl", left, mate)
        got(i, "hm")
        pass_on(i, "hfm", right, xm, tok, tok)
        pass_on(i, "hcr", right, mate)

    def stage_e2(i):
        got(i, "hfp", "hfm")
        pass_on(i, "hcf", x2 * 2 + core, mate)

    def stage_f(i):
        got(i, "hc", "hcl", "hcr", "hcf")
        if i == 0:
            dn_load.wait()
        for j in range(2):
            cols = pl.ds(j * width // 2, width // 2)
            part = jnp.dot(
                hid[i].reshape(rows * tok, feats), dn[:, cols], preferred_element_type=F32
            )
            part = (part * down_scale[:, cols]).astype(BF16)
            o_send[i, :, :, cols] = part.reshape(rows, tok, width // 2)
        for q, peer in enumerate(peers):
            send(i, f"o{q}", o_send.at[i, peer[0]], o_recv.at[i, q], peer)

    def stage_j(i):
        got(i, *[f"o{q}" for q in range(len(peers))])
        total = o_send[i, row].astype(F32)
        for q in range(len(peers)):
            total = total + o_recv[i, q].astype(F32)
        out[pl.ds(tok * i, tok), :] = total.astype(BF16)

    stages = {
        "A": stage_a, "B": stage_b, "C": stage_c, "D": stage_d, "E": stage_e,
        "e": stage_e2, "F": stage_f, "J": stage_j,
    }
    for words in ORDER:
        for word in words.split():
            name, piece, chunk = word
            if piece == ".":
                stages[name](int(chunk))
            else:
                stages[name](int(chunk), int(piece))
    for i in range(n):
        for copy in copies[i].values():
            copy.wait_send()


def body(act_quant, act_scale, gate_up_quant, gate_up_scale, down_quant, down_scale):
    local_rows, width = act_quant.shape
    feats = gate_up_quant.shape[2]
    rows = lax.axis_size("row")
    n, tok = CHUNKS, local_rows // CHUNKS
    block = 2 * tok
    any_spec = pl.BlockSpec(memory_space=pl.ANY)
    vmem_spec = pl.BlockSpec(memory_space=pltpu.VMEM)
    vmem = pltpu.VMEM
    return pl.pallas_call(
        kernel,
        out_shape=jax.ShapeDtypeStruct((local_rows, width), BF16),
        in_specs=[any_spec, vmem_spec, any_spec, vmem_spec, any_spec, vmem_spec],
        out_specs=vmem_spec,
        scratch_shapes=[
            vmem((n, rows, tok, width), BF16),
            vmem((2 * feats, width), BF16),
            vmem((feats, width), BF16),
            vmem((2, 4, 2, block, 2 * feats), F32),
            vmem((n, 4, block, 2 * feats), F32),
            vmem((n, block, 2 * feats), BF16),
            vmem((n, block, 2 * feats), BF16),
            vmem((n, block, 2 * feats), F32),
            vmem((n, block, 2 * feats), F32),
            vmem((n, block, 2 * feats), BF16),
            vmem((n, block, 2 * feats), BF16),
            vmem((n, block, 2 * feats), BF16),
            vmem((n, 8, block, feats), BF16),
            vmem((n, rows, tok, width), BF16),
            vmem((n, rows - 1, tok, width), BF16),
            vmem((128, 128), F32),
            pltpu.SemaphoreType.DMA((n + 5,)),
            pltpu.SemaphoreType.DMA((n, 54)),
            pltpu.SemaphoreType.DMA((n, 54)),
        ],
        compiler_params=pltpu.CompilerParams(
            collective_id=0, has_side_effects=True, vmem_limit_bytes=63_000_000
        ),
        name="gated_ffn",
    )(
        act_quant, act_scale.reshape(8, 128),
        jnp.swapaxes(gate_up_quant, 1, 2).reshape(2 * feats, width), gate_up_scale,
        down_quant, down_scale.reshape(1, width),
    )


def solution(mesh):
    in_specs = (
        P("row", "col"),
        P(),
        P(None, "col", "row"),
        P(None, "row"),
        P("row", "col"),
        P("col"),
    )
    out_specs = P("row", "col")
    return jax.shard_map(body, mesh=mesh, in_specs=in_specs, out_specs=out_specs, check_vma=False)
```

time: 256 us -> 91.7 us (0.36)
  waiting for transfers between devices: 115 us -> 0 us
  blocking collectives: 94.8 us -> 0 us
  Pallas kernels: 0 us -> 89.5 us
  matrix products: 18.7 us -> 0 us
  between operations: 13.5 us -> 0.01 us
  other arithmetic: 12.1 us -> 0 us
    all_to_all x2 -> x0, blocking collectives: 94.8 us -> none  [the longest x1 58.2 us: sent_and_summed(): lax.all_to_all(tiles, axis, split_axis=0, concat_axis=0, tiled=True)]
    pallas_call x0 -> x1, Pallas kernels: none -> 89.5 us  [body(): pl.pallas_call(kernel, out_shape=jax.ShapeDtypeStruct((local_rows, width)...]
    reduce_scatter x1 -> x0, waiting for transfers between devices: 81.1 us -> none  [body(): lax.psum_scatter(jnp.concatenate([gate_part, up_part], axis=1), 'col', sc...]
    all_gather x1 -> x0, waiting for transfers between devices: 33.6 us -> none  [body(): hidden = lax.all_gather(hidden, 'col', axis=0, tiled=True)]
    dot_general x3 -> x0, matrix products: 18.7 us -> none  [the longest x1 7.97 us: body(): jnp.dot(hidden, down_quant, preferred_element_type=jnp.float32)]
    concatenate x1 -> x0, other arithmetic: 5.96 us -> none  [body(): jnp.concatenate([gate_part, up_part], axis=1)]
    reduce_sum x1 -> x0, other arithmetic: 3.15 us -> none  [sent_and_summed(): return arrived.sum(axis=0)]
    convert_element_type x1 -> x0, other arithmetic: 3 us -> none  [body(): hidden = (jax.nn.silu(gate_val) * up_val).astype(jnp.bfloat16)]
  transfers between devices with their start and end apart: 2 -> 0, of which waited for: 2 -> 0; matrix products, arithmetic and copies ran while one was open for 0% -> 0% of each run, Pallas kernels for 0% -> 0%
where the time goes in v1:
time: 91.7 us; the launch traced here: 91.1 us
  Pallas kernels  89.5 us (98%)
  local copies, waits for them, and re-layouts  1.57 us (2%)
    pallas_call x1, Pallas kernels, body(): pl.pallas_call(kernel, out_shape=jax.ShapeDtypeStruct((local_rows, width)...  89.5 us

profile of v1, /device:TPU:0, one launch (start us, length us, event | category | flops | bytes accessed | tf_op | source)
XLA Modules:
  0.0 91.1 jit_solution(360737045675788826)
XLA Ops:
  0.0 89.5 %gated_ffn.1 = bf16[64,1024]{1,0:T(8,128)(2,1)} custom-call(bf16[64,1024]{1,0:T(8,128)(2,1)} %act_hbm.1, f32[8,128]{1,0:T(8,128)} %bitcast.6, bf16[3696,1024]{1,0:T(8,128)(2,1)} %bitcast.5, f32[2,1848]{1,0:T(2,128)} %gate_up_scale.1, bf16[1848,1024]{1,0:T(8,128)(2,1)} %down_hbm.1, f32[1,1024]{1,0:T(1,128)} %bitcast.7), custom_call_target="tpu_custom_call" | custom-call | tf_op jit(solution)/shard_map/gated_ffn/pallas_call | solution.py:207
  89.5 1.6 %copy.8 = bf16[64,1024]{1,0:T(8,128)(2,1)} copy(bf16[64,1024]{1,0:T(8,128)(2,1)} %gated_ffn.1) | data formatting | bytes 262144

commit v2 on v1

v2 whole, which is shorter than its diff:
```python
import jax
import jax.numpy as jnp
from jax import lax
from jax.experimental import pallas as pl
from jax.experimental.pallas import tpu as pltpu
from jax.sharding import PartitionSpec as P

MESH = pl.DeviceIdType.MESH
CHUNKS = 4
F32 = jnp.float32
BF16 = jnp.bfloat16
OFFSETS = [(a, b) for a in range(4) for b in range(4) if a or b]
PIECES = ((0, 1024, 0), (1024, 768, 0), (1792, 1024, 1), (2816, 880, 1))
UNITS = ((0, (0, 1)), (1, (0, 1)), (2, (0, 1)), (3, (0,)), (3, (1,)))
ORDER = (
    "p.0 q.0 p.1 r.0", "q.1 s.0 r.1 t.0", "A00 A10 A20 A30", "B00 B10 B20 B30",
    "s.1 g.2 t.1 A01", "A11 C00 C10 A21", "A31 C20 C30 B01", "B11 B21 B31 g.3",
    "A02 A12 A22 A32", "D.0 C01 C11 C21", "C31 B02 B12 B22", "B32 E.0 A03 A13",
    "A23 A33 D.1 C02", "C12 C22 C32 B03", "B13 B23 B33 E.1", "F.0 D.2 C03 C13",
    "C23 C33 B04 B14", "B24 B34 E.2 F.1", "D.3 C04 C14 C24", "C34 F.2 E.3 D.4",
    "J.0 F.3 E.4 J.1", "F.4 J.2 J.3 J.4",
)


def kernel(
    act_hbm, act_scale, gate_up_hbm, gate_up_scale, down_hbm, down_scale, out,
    act, w, dn, acc, pair, first, direct, merge, own, first_in, left_in, right_in,
    hid, o_send, o_recv, scale, load_sem, send_sem, recv_sem, out_sem,
):
    n, rows, tok, width = act.shape
    half = width // 2
    feats = hid.shape[4]
    row, col = lax.axis_index("row"), lax.axis_index("col")
    z, y, x, core = row // 4, row % 4, col // 2, col % 2
    x1, x2, x3 = (x + 1) % 4, (x + 2) % 4, (x + 3) % 4
    y1, y2, y3 = (y + 1) % 4, (y + 2) % 4, (y + 3) % 4
    z1, z3 = (z + 1) % 4, (z + 3) % 4
    xp, xm = (row, x1 * 2 + core), (row, x3 * 2 + core)
    yp, ym = (z * 4 + y1, col), (z * 4 + y3, col)
    zp, zm = (z1 * 4 + y, col), (z3 * 4 + y, col)
    mate = (row, x * 2 + 1 - core)
    peers = [((z + a) % 4 * 4 + (y + b) % 4, col) for a, b in OFFSETS]

    def load(src, dst, index):
        copy = pltpu.make_async_copy(src, dst, load_sem.at[index])
        copy.start()
        return copy

    own_loads = [
        load(act_hbm.at[pl.ds(tok * i, tok)], act.at[i, row], i) for i in range(n)
    ]
    w_loads = [
        load(gate_up_hbm.at[pl.ds(s, m)], w.at[pl.ds(s, m)], n + p)
        for p, (s, m, _) in enumerate(PIECES)
    ]
    dn_load = load(down_hbm, dn.at[core], n + len(PIECES))

    names, spare = {}, iter(range(176, 256))
    copies = {}

    def send(key, name, src, dst, device):
        index = names.setdefault((key, name), len(names))
        copy = pltpu.make_async_remote_copy(
            src_ref=src, dst_ref=dst, send_sem=send_sem.at[index],
            recv_sem=recv_sem.at[index],
            device_id=device, device_id_type=MESH,
        )
        copy.start()
        copies[key, name] = copy

    def got(key, *which):
        for name in which:
            copies[key, name].wait_recv()

    barrier = pltpu.get_barrier_semaphore()
    near = (xp, xm, mate, yp, ym, zp, zm)
    for device in near:
        pl.semaphore_signal(barrier, inc=1, device_id=device, device_id_type=MESH)

    lane = lax.broadcasted_iota(jnp.int32, (128, 128), 1)
    line = lax.broadcasted_iota(jnp.int32, (128, 128), 0)
    mine = jnp.broadcast_to(act_scale[pl.ds(col, 1), :], (128, 128))
    column = jnp.sum(jnp.where(lane == line, mine, 0.0), axis=1, keepdims=True)
    scale[...] = jnp.broadcast_to(column, (128, 128))

    pl.semaphore_wait(barrier, len(near))

    def r_at(zz, yy):
        return zz * 4 + yy

    def spread(i, name, block):
        send(("a", i), name + "p", act.at[i, block], act.at[i, block], zp)
        send(("a", i), name + "m", act.at[i, block], act.at[i, block], zm)

    def forward(i, name, yy):
        got(("a", i), name + "p", name + "m")
        low = act.at[i, r_at(z3, yy), :, pl.ds(0, half)]
        high = act.at[i, r_at(z1, yy), :, pl.ds(half, half)]
        send(("a", i), "f" + name + "p", low, low, zp)
        send(("a", i), "f" + name + "m", high, high, zm)

    def stage_p(i):
        own_loads[i].wait()
        send(("a", i), "y1p", act.at[i, row], act.at[i, row], yp)
        send(("a", i), "y1m", act.at[i, row], act.at[i, row], ym)
        spread(i, "za", row)

    def stage_q(i):
        got(("a", i), "y1p", "y1m")
        low = act.at[i, r_at(z, y3), :, pl.ds(0, half)]
        high = act.at[i, r_at(z, y1), :, pl.ds(half, half)]
        send(("a", i), "y2p", low, low, yp)
        send(("a", i), "y2m", high, high, ym)
        spread(i, "zb", r_at(z, y3))
        spread(i, "zc", r_at(z, y1))

    def stage_r(i):
        got(("a", i), "y2p", "y2m")
        spread(i, "zd", r_at(z, y2))
        forward(i, "za", y)

    def stage_s(i):
        forward(i, "zb", y3)
        forward(i, "zc", y1)
        forward(i, "zd", y2)
        if i == 0:
            send("dn", "", down_hbm, dn.at[core], mate)

    def stage_t(i):
        got(("a", i), *["fz" + k + d for k in "abcd" for d in "pm"])

    def stage_g(i):
        own_loads[i].wait()
        for q, peer in enumerate(peers):
            send(("a", i), f"a{q}", act.at[i, row], act.at[i, row], peer)

    def stage_a(i, p):
        start, size, _ = PIECES[p]
        cols = pl.ds(start, size)
        if p == 0:
            if (("a", i), "a0") in copies:
                got(("a", i), *[f"a{q}" for q in range(len(peers))])
            if i >= 2:
                for q in range(len(PIECES)):
                    copies.pop((("p", i - 2), q)).wait_send()
        if i == 0:
            w_loads[p].wait()
        part = lax.dot_general(
            act[i].reshape(rows * tok, width), w[cols, :], (((1,), (1,)), ((), ())),
            preferred_element_type=F32,
        )
        s = i % 2
        acc[s, :, :, :, :, cols] = part.reshape(4, 2, 2, tok, size)
        send(
            ("p", i), p, acc.at[s, :, 1 - core, :, :, cols], pair.at[i, :, :, :, cols], mate
        )

    def slots(u):
        hs = UNITS[u][1]
        return pl.ds(hs[0], len(hs))

    def stage_b(u, p):
        i, hs = UNITS[u]
        start, size, side = PIECES[p]
        cols = pl.ds(start, size)
        s, sl = i % 2, slots(u)

        def both(d):
            j = pl.ds(0, 2) if len(hs) == 2 else pl.ds((hs[0] + d) % 2, 1)
            return acc[s, d, core, j, :, cols] + pair[i, d, j, :, cols]

        if hs[0] == 0:
            got(("p", i), p)
        near_dev, far_dev = (xm, xp) if side == 0 else (xp, xm)
        near_x, far_x = (x3, x1) if side == 0 else (x1, x3)
        landing = right_in if side == 0 else left_in
        first[i, sl, :, cols] = both(x2).astype(BF16)
        send(u, f"s{p}", first.at[i, sl, :, cols], first_in.at[i, sl, :, cols], far_dev)
        direct[i, sl, :, cols] = both(near_x).astype(BF16)
        send(u, f"d{p}", direct.at[i, sl, :, cols], landing.at[i, sl, :, cols], near_dev)
        merge[i, sl, :, cols] = both(far_x)
        own[i, sl, :, cols] = both(x)

    def stage_c(u, p):
        i, sl = UNITS[u][0], slots(u)
        start, size, side = PIECES[p]
        cols = pl.ds(start, size)
        far_dev, landing = (xp, left_in) if side == 0 else (xm, right_in)
        got(u, f"s{p}")
        copies.pop((u, f"s{p}")).wait_send()
        total = merge[i, sl, :, cols] + first_in[i, sl, :, cols].astype(F32)
        first[i, sl, :, cols] = total.astype(BF16)
        send(u, f"m{p}", first.at[i, sl, :, cols], landing.at[i, sl, :, cols], far_dev)

    def pass_on(u, name, d, device, start=0, size=None):
        i, sl = UNITS[u][0], slots(u)
        part = hid.at[i, sl, d, :, pl.ds(start, size or feats)]
        send(u, name, part, part, device)

    def stage_d(u):
        i, hs = UNITS[u]
        sl = slots(u)
        got(u, *[kind + str(p) for kind in "dm" for p in range(len(PIECES))])
        total = own[i, sl] + left_in[i, sl].astype(F32) + right_in[i, sl].astype(F32)
        total = total.reshape(len(hs) * tok, 2 * feats)
        if len(hs) == 2:
            token = jnp.concatenate(
                [scale[pl.ds(tok * i, tok), 0:1], scale[pl.ds(64 + tok * i, tok), 0:1]], axis=0
            )
        else:
            begin = pl.multiple_of((hs[0] + x) % 2 * 64 + tok * i, tok)
            token = scale[pl.ds(begin, tok), 0:1]
        gate = total[:, :feats] * token * gate_up_scale[0:1, :]
        up = total[:, feats:] * token * gate_up_scale[1:2, :]
        value = (gate / (1.0 + jnp.exp(-gate)) * up).astype(BF16)
        hid[i, sl, x] = value.reshape(len(hs), tok, feats)
        pass_on(u, "hp", x, xp)
        pass_on(u, "hm", x, xm)

    split = feats // 256 * 128

    def stage_e(u):
        got(u, "hp")
        pass_on(u, "hfp", x3, xp, 0, split)
        got(u, "hm")
        pass_on(u, "hfm", x1, xm, split, feats - split)

    def is_self(a, to_y, to_core):
        return (to_y == y) & (to_core == core) if a == 0 else None

    def unless(skip, todo):
        if skip is None:
            todo()
        else:
            pl.when(jnp.logical_not(skip))(todo)

    out_sends = []

    def stage_f(u):
        i, hs = UNITS[u]
        sl = slots(u)
        got(u, "hfp", "hfm")
        if i == 0:
            dn_load.wait()
            got("dn", "")
        count = len(hs)
        for h in range(2):
            for c in range(2):
                cols = pl.ds(c * half, half)
                part = jnp.dot(
                    hid[i, sl].reshape(count * 4 * tok, feats), dn[h, :, cols],
                    preferred_element_type=F32,
                )
                o_send[i, h, sl, :, :, cols] = part.astype(BF16).reshape(count, 4, tok, half)
            for a in range(4):
                d = (z + a) % 4
                for slot in hs:
                    j = slot if count == 2 else (slot + d) % 2
                    to_y = 2 * core + j
                    skip = is_self(a, to_y, h)
                    index, device = a * 4 + y, (d * 4 + to_y, x * 2 + h)

                    def build(h=h, slot=slot, d=d, device=device, index=index, k=next(spare)):
                        return pltpu.make_async_remote_copy(
                            src_ref=o_send.at[i, h, slot, d], dst_ref=o_recv.at[i, index],
                            send_sem=send_sem.at[k], recv_sem=out_sem.at[i, index],
                            device_id=device, device_id_type=MESH,
                        )

                    unless(skip, lambda build=build: build().start())
                    out_sends.append((skip, build))

    def stage_j(u):
        i, hs = UNITS[u]
        mine = y // 2 == core
        own_slot = y % 2 if len(hs) == 2 else hs[0]

        def take():
            @pl.when(mine)
            def _():
                o_recv[i, y] = o_send[i, core, own_slot, z]

            for q in range(16):
                def wait(q=q):
                    pltpu.make_async_remote_copy(
                        src_ref=o_recv.at[i, q], dst_ref=o_recv.at[i, q],
                        send_sem=send_sem.at[0], recv_sem=out_sem.at[i, q],
                        device_id=mate, device_id_type=MESH,
                    ).wait_recv()

                unless((q == y) & mine if q < 4 else None, wait)
            total = o_recv[i, 0].astype(F32)
            for q in range(1, 16):
                total = total + o_recv[i, q].astype(F32)
            out[pl.ds(tok * i, tok), :] = (total * down_scale[...]).astype(BF16)

        if len(hs) == 2:
            take()
        else:
            pl.when((y + z) % 2 == hs[0])(take)

    stages = {
        "p": stage_p, "q": stage_q, "r": stage_r, "s": stage_s, "t": stage_t,
        "g": stage_g, "A": stage_a, "B": stage_b, "C": stage_c, "D": stage_d,
        "E": stage_e, "F": stage_f, "J": stage_j,
    }
    for words in ORDER:
        for word in words.split():
            name, piece, chunk = word
            if piece == ".":
                stages[name](int(chunk))
            else:
                stages[name](int(chunk), int(piece))
    for copy in copies.values():
        copy.wait_send()
    for skip, build in out_sends:
        unless(skip, lambda build=build: build().wait_send())


def body(act_quant, act_scale, gate_up_quant, gate_up_scale, down_quant, down_scale):
    local_rows, width = act_quant.shape
    feats = gate_up_quant.shape[2]
    rows = lax.axis_size("row")
    n, tok = CHUNKS, local_rows // CHUNKS
    any_spec = pl.BlockSpec(memory_space=pl.ANY)
    vmem_spec = pl.BlockSpec(memory_space=pltpu.VMEM)
    vmem = pltpu.VMEM
    return pl.pallas_call(
        kernel,
        out_shape=jax.ShapeDtypeStruct((local_rows, width), BF16),
        in_specs=[any_spec, vmem_spec, any_spec, vmem_spec, any_spec, vmem_spec],
        out_specs=vmem_spec,
        scratch_shapes=[
            vmem((n, rows, tok, width), BF16),
            vmem((2 * feats, width), BF16),
            vmem((2, feats, width), BF16),
            vmem((2, 4, 2, 2, tok, 2 * feats), F32),
            vmem((n, 4, 2, tok, 2 * feats), F32),
            vmem((n, 2, tok, 2 * feats), BF16),
            vmem((n, 2, tok, 2 * feats), BF16),
            vmem((n, 2, tok, 2 * feats), F32),
            vmem((n, 2, tok, 2 * feats), F32),
            vmem((n, 2, tok, 2 * feats), BF16),
            vmem((n, 2, tok, 2 * feats), BF16),
            vmem((n, 2, tok, 2 * feats), BF16),
            vmem((n, 2, 4, tok, feats), BF16),
            vmem((n, 2, 2, 4, tok, width), BF16),
            vmem((n, rows, tok, width), BF16),
            vmem((128, 128), F32),
            pltpu.SemaphoreType.DMA((n + 5,)),
            pltpu.SemaphoreType.DMA((256,)),
            pltpu.SemaphoreType.DMA((176,)),
            pltpu.SemaphoreType.DMA((n, 16)),
        ],
        compiler_params=pltpu.CompilerParams(
            collective_id=0, has_side_effects=True, vmem_limit_bytes=63_000_000
        ),
        name="gated_ffn",
    )(
        act_quant, act_scale.reshape(8, 128),
        jnp.swapaxes(gate_up_quant, 1, 2).reshape(2 * feats, width), gate_up_scale,
        down_quant, down_scale.reshape(1, width),
    )


def solution(mesh):
    in_specs = (
        P("row", "col"),
        P(),
        P(None, "col", "row"),
        P(None, "row"),
        P("row", "col"),
        P("col"),
    )
    out_specs = P("row", "col")
    return jax.shard_map(body, mesh=mesh, in_specs=in_specs, out_specs=out_specs, check_vma=False)
```

time: 91.7 us -> 96.9 us (1.057)
  Pallas kernels: 89.5 us -> 95.1 us
    pallas_call x1, Pallas kernels: 89.5 us -> 95.1 us  [body(): pl.pallas_call(kernel, out_shape=jax.ShapeDtypeStruct((local_rows, width)...]
where the time goes in v2:
time: 96.9 us; the launch traced here: 96.7 us
  Pallas kernels  95.1 us (98%)
  local copies, waits for them, and re-layouts  1.57 us (2%)
    pallas_call x1, Pallas kernels, body(): pl.pallas_call(kernel, out_shape=jax.ShapeDtypeStruct((local_rows, width)...  95.1 us

profile of v2, /device:TPU:0, one launch (start us, length us, event | category | flops | bytes accessed | tf_op | source)
XLA Modules:
  0.0 96.7 jit_solution(7625738522330973836)
XLA Ops:
  0.0 95.1 %gated_ffn.1 = bf16[64,1024]{1,0:T(8,128)(2,1)} custom-call(bf16[64,1024]{1,0:T(8,128)(2,1)} %act_hbm.1, f32[8,128]{1,0:T(8,128)} %bitcast.6, bf16[3696,1024]{1,0:T(8,128)(2,1)} %bitcast.5, f32[2,1848]{1,0:T(2,128)} %gate_up_scale.1, bf16[1848,1024]{1,0:T(8,128)(2,1)} %down_hbm.1, f32[1,1024]{1,0:T(1,128)} %bitcast.7), custom_call_target="tpu_custom_call" | custom-call | tf_op jit(solution)/shard_map/gated_ffn/pallas_call | solution.py:328
  95.1 1.6 %copy.8 = bf16[64,1024]{1,0:T(8,128)(2,1)} copy(bf16[64,1024]{1,0:T(8,128)(2,1)} %gated_ffn.1) | data formatting | bytes 262144

commit v3 on v2

v3 whole, which is shorter than its diff:
```python
import jax
import jax.numpy as jnp
from jax import lax
from jax.experimental import pallas as pl
from jax.experimental.pallas import tpu as pltpu
from jax.sharding import PartitionSpec as P

MESH = pl.DeviceIdType.MESH
CHUNKS = 4
F32 = jnp.float32
BF16 = jnp.bfloat16
NEAR = (((0, 0), (0, 1)), ((0, 3), (1, 0)), ((3, 0), (1, 1)), ((3, 3), (1, 3)))
FAR = (((3, 1), (0, 2)), ((2, 0), (1, 2)), ((3, 2), (2, 1)), ((2, 3), (2, 2)))
PLACES = [(d, c, h) for h in range(2) for d in range(4) for c in range(2)]
PIECES = ((0, 1024, 0), (1024, 768, 0), (1792, 1024, 1), (2816, 880, 1))
GROUPS = ((0, (0,)), (0, (1,)), (1, (0, 1)), (2, (0, 1)), (3, (0, 1)))
UNITS = ((0, (0,)), (0, (1,)), (1, (1,)), (1, (0,)), (2, (1,)), (2, (0,)), (3, (1,)), (3, (0,)))
ORDER = (
    "A00 A10 A20 A30", "A01 B00 A11 B10", "B20 A21 B01 B30", "A31 B11 C00 C10", "B21 B31 C20 A02",
    "C30 C01 C11 C21", "A12 C31 B02 B03", "D.0 A22 A32 B12", "D.1 A03 B22 A13", "C02 B32 B13 C12",
    "E.0 B04 A23 B14", "C22 B23 C03 B05", "E.1 B33 A33 A04", "C13 B15 A14 A24", "B24 A34 B06 C32",
    "B25 B34 B16 C05", "C04 B26 C14 C23", "C33 B36 C24 C34", "D.2 F.1 B35 C06", "C16 C26 C36 D.4",
    "E.2 B07 F.0 C15", "C25 B17 D.6 E.4", "B27 C35 F.2 C07", "B37 C17 E.6 D.3", "F.4 C27 C37 J.0",
    "D.5 F.6 E.3 D.7", "E.5 F.3 E.7 F.5", "F.7 J.2 J.1 J.3",
)


def kernel(
    act_hbm, act_scale, gate_up_hbm, gate_up_scale, down_hbm, down_scale, out,
    act, w, dn, acc, pair, first, direct, merge, own, first_in, left_in, right_in,
    hid, o_send, o_recv, scale, load_sem, send_sem, recv_sem, out_sem,
    act_send, act_recv,
):
    n, tok, width = act.shape[0], act.shape[4], act.shape[5]
    half = width // 2
    feats = hid.shape[4]
    row, col = lax.axis_index("row"), lax.axis_index("col")
    z, y, x, core = row // 4, row % 4, col // 2, col % 2
    x1, x2, x3 = (x + 1) % 4, (x + 2) % 4, (x + 3) % 4
    xp, xm = (row, x1 * 2 + core), (row, x3 * 2 + core)
    mate = (row, x * 2 + 1 - core)

    def offset(d, c, h):
        return (NEAR, FAR)[h][d][c]

    def row_of(d, h, axis):
        own = (z, y)[axis]
        value = 0
        if isinstance(d, int):
            return (own + jnp.where(core == 0, *[offset(d, c, h)[axis] for c in range(2)])) % 4
        for k in range(4):
            pair_of = [offset(k, c, h)[axis] for c in range(2)]
            value = value + jnp.where(d == k, jnp.where(core == 0, *pair_of), 0)
        return (own + value) % 4

    def load(src, dst, index):
        copy = pltpu.make_async_copy(src, dst, load_sem.at[index])
        copy.start()
        return copy

    own_loads = [
        load(act_hbm.at[pl.ds(tok * i, tok)], act.at[i, 0, 0, 0], i) for i in range(n)
    ]
    w_loads = [
        load(gate_up_hbm.at[pl.ds(s, m)], w.at[pl.ds(s, m)], n + p)
        for p, (s, m, _) in enumerate(PIECES)
    ]
    dn_load = load(down_hbm, dn.at[core], n + len(PIECES))

    names, spare = {}, iter(range(149, 213))
    copies = {}

    def send(key, name, src, dst, device):
        index = names.setdefault((key, name), len(names))
        copy = pltpu.make_async_remote_copy(
            src_ref=src, dst_ref=dst, send_sem=send_sem.at[index],
            recv_sem=recv_sem.at[index],
            device_id=device, device_id_type=MESH,
        )
        copy.start()
        copies[key, name] = copy

    def got(key, *which):
        for name in which:
            copies[key, name].wait_recv()

    barrier = pltpu.get_barrier_semaphore()
    near = [xp, xm, mate] + [
        ((z + a) % 4 * 4 + (y + b) % 4, col) for a in range(4) for b in range(4) if a or b
    ]
    for device in near:
        pl.semaphore_signal(barrier, inc=1, device_id=device, device_id_type=MESH)

    lane = lax.broadcasted_iota(jnp.int32, (128, 128), 1)
    line = lax.broadcasted_iota(jnp.int32, (128, 128), 0)
    begins = []
    for h in range(2):
        source = row_of(x, h, 0) * 4 + row_of(x, h, 1)
        mine = jnp.broadcast_to(act_scale[pl.ds(source // 2, 1), :], (128, 128))
        column = jnp.sum(jnp.where(lane == line, mine, 0.0), axis=1, keepdims=True)
        scale[h] = jnp.broadcast_to(column, (128, 128))
        begins.append(source % 2 * 64)

    pl.semaphore_wait(barrier, len(near))

    def to_rows(i):
        for q, (d, c, h) in enumerate(PLACES[1:]):
            a, b = offset(d, c, h)
            yield h, pltpu.make_async_remote_copy(
                src_ref=act.at[i, 0, 0, 0], dst_ref=act.at[i, d, c, h],
                send_sem=act_send.at[i, q], recv_sem=act_recv.at[i, q],
                device_id=((z - a + 4) % 4 * 4 + (y - b + 4) % 4, col), device_id_type=MESH,
            )

    for i in range(n):
        own_loads[i].wait()
        for _, copy in to_rows(i):
            copy.start()
    send("dn", "", down_hbm, dn.at[core], mate)

    def stage_a(g, p):
        i, hs = GROUPS[g]
        start, size, _ = PIECES[p]
        cols, sl = pl.ds(start, size), pl.ds(hs[0], len(hs))
        if p == 0:
            for h, copy in to_rows(i):
                if h in hs:
                    copy.wait_recv()
            if g >= 2:
                for q in range(len(PIECES)):
                    copies.pop((("p", g - 2), q)).wait_send()
        if g == 0:
            w_loads[p].wait()
        part = lax.dot_general(
            act[i, :, :, sl].reshape(8 * len(hs) * tok, width), w[cols, :],
            (((1,), (1,)), ((), ())), preferred_element_type=F32,
        )
        s = g % 2
        acc[s, :, :, sl, :, cols] = part.reshape(4, 2, len(hs), tok, size)
        send(
            ("p", g), p, acc.at[s, :, 1 - core, sl, :, cols], pair.at[i, :, sl, :, cols], mate
        )

    paired = set()

    def slots(u):
        hs = UNITS[u][1]
        return pl.ds(hs[0], len(hs))

    def stage_b(u, p):
        i, hs = UNITS[u]
        start, size, side = PIECES[p]
        cols = pl.ds(start, size)
        g = [k for k, (c, rows) in enumerate(GROUPS) if c == i and hs[0] in rows][0]
        s, sl = g % 2, slots(u)

        def both(d):
            return acc[s, d, core, sl, :, cols] + pair[i, d, sl, :, cols]

        if (g, p) not in paired:
            paired.add((g, p))
            got(("p", g), p)
        near_dev, far_dev = (xm, xp) if side == 0 else (xp, xm)
        near_x, far_x = (x3, x1) if side == 0 else (x1, x3)
        landing = right_in if side == 0 else left_in
        first[i, sl, :, cols] = both(x2).astype(BF16)
        send(u, f"s{p}", first.at[i, sl, :, cols], first_in.at[i, sl, :, cols], far_dev)
        direct[i, sl, :, cols] = both(near_x).astype(BF16)
        send(u, f"d{p}", direct.at[i, sl, :, cols], landing.at[i, sl, :, cols], near_dev)
        merge[i, sl, :, cols] = both(far_x)
        own[i, sl, :, cols] = both(x)

    def stage_c(u, p):
        i, sl = UNITS[u][0], slots(u)
        start, size, side = PIECES[p]
        cols = pl.ds(start, size)
        far_dev, landing = (xp, left_in) if side == 0 else (xm, right_in)
        got(u, f"s{p}")
        copies.pop((u, f"s{p}")).wait_send()
        total = merge[i, sl, :, cols] + first_in[i, sl, :, cols].astype(F32)
        first[i, sl, :, cols] = total.astype(BF16)
        send(u, f"m{p}", first.at[i, sl, :, cols], landing.at[i, sl, :, cols], far_dev)

    def pass_on(u, name, d, device, start=0, size=None):
        i, sl = UNITS[u][0], slots(u)
        part = hid.at[i, sl, d, :, pl.ds(start, size or feats)]
        send(u, name, part, part, device)

    def stage_d(u):
        i, hs = UNITS[u]
        sl = slots(u)
        got(u, *[kind + str(p) for kind in "dm" for p in range(len(PIECES))])
        total = own[i, sl] + left_in[i, sl].astype(F32) + right_in[i, sl].astype(F32)
        total = total.reshape(len(hs) * tok, 2 * feats)
        token = jnp.concatenate(
            [scale[h, pl.ds(pl.multiple_of(begins[h] + tok * i, tok), tok), 0:1] for h in hs],
            axis=0,
        )
        gate = total[:, :feats] * token * gate_up_scale[0:1, :]
        up = total[:, feats:] * token * gate_up_scale[1:2, :]
        value = (gate / (1.0 + jnp.exp(-gate)) * up).astype(BF16)
        hid[i, sl, x] = value.reshape(len(hs), tok, feats)
        pass_on(u, "hp", x, xp)
        pass_on(u, "hm", x, xm)

    split = feats // 256 * 128

    def stage_e(u):
        got(u, "hp")
        pass_on(u, "hfp", x3, xp, 0, split)
        got(u, "hm")
        pass_on(u, "hfm", x1, xm, split, feats - split)

    def unless(skip, todo):
        if skip is None:
            todo()
        else:
            pl.when(jnp.logical_not(skip))(todo)

    out_sends = []

    def stage_f(u):
        i, hs = UNITS[u]
        sl = slots(u)
        got(u, "hfp", "hfm")
        if not out_sends:
            dn_load.wait()
            got("dn", "")
        count = len(hs)
        for h in range(2):
            for c in range(2):
                cols = pl.ds(c * half, half)
                part = jnp.dot(
                    hid[i, sl].reshape(count * 4 * tok, feats), dn[h, :, cols],
                    preferred_element_type=F32,
                )
                o_send[i, h, sl, :, :, cols] = part.astype(BF16).reshape(count, 4, tok, half)
            for slot in hs:
                for d in range(4):
                    device = (row_of(d, slot, 0) * 4 + row_of(d, slot, 1), x * 2 + h)
                    index = slot * 8 + d * 2 + core
                    skip = (core == 0) if (d, slot, h) == (0, 0, 0) else None

                    def build(h=h, slot=slot, d=d, device=device, index=index, k=next(spare)):
                        return pltpu.make_async_remote_copy(
                            src_ref=o_send.at[i, h, slot, d], dst_ref=o_recv.at[i, index],
                            send_sem=send_sem.at[k], recv_sem=out_sem.at[i, index],
                            device_id=device, device_id_type=MESH,
                        )

                    unless(skip, lambda build=build: build().start())
                    out_sends.append((skip, build))

    def stage_j(i):
        @pl.when(core == 0)
        def _():
            o_recv[i, 0] = o_send[i, 0, 0, 0]

        for q in range(16):
            def wait(q=q):
                pltpu.make_async_remote_copy(
                    src_ref=o_recv.at[i, q], dst_ref=o_recv.at[i, q],
                    send_sem=send_sem.at[0], recv_sem=out_sem.at[i, q],
                    device_id=mate, device_id_type=MESH,
                ).wait_recv()

            unless(core == 0 if q == 0 else None, wait)
        total = o_recv[i, 0].astype(F32)
        for q in range(1, 16):
            total = total + o_recv[i, q].astype(F32)
        out[pl.ds(tok * i, tok), :] = (total * down_scale[...]).astype(BF16)

    stages = {
        "A": stage_a, "B": stage_b, "C": stage_c, "D": stage_d,
        "E": stage_e, "F": stage_f, "J": stage_j,
    }
    for words in ORDER:
        for word in words.split():
            name, piece, chunk = word
            if piece == ".":
                stages[name](int(chunk))
            else:
                stages[name](int(chunk), int(piece))
    for copy in copies.values():
        copy.wait_send()
    for i in range(n):
        for _, copy in to_rows(i):
            copy.wait_send()
    for skip, build in out_sends:
        unless(skip, lambda build=build: build().wait_send())


def body(act_quant, act_scale, gate_up_quant, gate_up_scale, down_quant, down_scale):
    local_rows, width = act_quant.shape
    feats = gate_up_quant.shape[2]
    rows = lax.axis_size("row")
    n, tok = CHUNKS, local_rows // CHUNKS
    any_spec = pl.BlockSpec(memory_space=pl.ANY)
    vmem_spec = pl.BlockSpec(memory_space=pltpu.VMEM)
    vmem = pltpu.VMEM
    return pl.pallas_call(
        kernel,
        out_shape=jax.ShapeDtypeStruct((local_rows, width), BF16),
        in_specs=[any_spec, vmem_spec, any_spec, vmem_spec, any_spec, vmem_spec],
        out_specs=vmem_spec,
        scratch_shapes=[
            vmem((n, 4, 2, 2, tok, width), BF16),
            vmem((2 * feats, width), BF16),
            vmem((2, feats, width), BF16),
            vmem((2, 4, 2, 2, tok, 2 * feats), F32),
            vmem((n, 4, 2, tok, 2 * feats), F32),
            vmem((n, 2, tok, 2 * feats), BF16),
            vmem((n, 2, tok, 2 * feats), BF16),
            vmem((n, 2, tok, 2 * feats), F32),
            vmem((n, 2, tok, 2 * feats), F32),
            vmem((n, 2, tok, 2 * feats), BF16),
            vmem((n, 2, tok, 2 * feats), BF16),
            vmem((n, 2, tok, 2 * feats), BF16),
            vmem((n, 2, 4, tok, feats), BF16),
            vmem((n, 2, 2, 4, tok, width), BF16),
            vmem((n, rows, tok, width), BF16),
            vmem((2, 128, 128), F32),
            pltpu.SemaphoreType.DMA((n + 5,)),
            pltpu.SemaphoreType.DMA((213,)),
            pltpu.SemaphoreType.DMA((149,)),
            pltpu.SemaphoreType.DMA((n, 16)),
            pltpu.SemaphoreType.DMA((n, 15)),
            pltpu.SemaphoreType.DMA((n, 15)),
        ],
        compiler_params=pltpu.CompilerParams(
            collective_id=0, has_side_effects=True, vmem_limit_bytes=63_000_000
        ),
        name="gated_ffn",
    )(
        act_quant, act_scale.reshape(8, 128),
        jnp.swapaxes(gate_up_quant, 1, 2).reshape(2 * feats, width), gate_up_scale,
        down_quant, down_scale.reshape(1, width),
    )


def solution(mesh):
    in_specs = (
        P("row", "col"),
        P(),
        P(None, "col", "row"),
        P(None, "row"),
        P("row", "col"),
        P("col"),
    )
    out_specs = P("row", "col")
    return jax.shard_map(body, mesh=mesh, in_specs=in_specs, out_specs=out_specs, check_vma=False)
```

time: 96.9 us -> 87.3 us (0.901); the launches traced: 96.7 us -> 85.7 us
  Pallas kernels: 95.1 us -> 84.1 us
    pallas_call x1, Pallas kernels: 95.1 us -> 84.1 us  [body(): pl.pallas_call(kernel, out_shape=jax.ShapeDtypeStruct((local_rows, width)...]
where the time goes in v3:
time: 87.3 us; the launch traced here: 85.7 us
  Pallas kernels  84.1 us (96%)
  local copies, waits for them, and re-layouts  1.57 us (2%)
    pallas_call x1, Pallas kernels, body(): pl.pallas_call(kernel, out_shape=jax.ShapeDtypeStruct((local_rows, width)...  84.1 us

profile of v3, /device:TPU:0, one launch (start us, length us, event | category | flops | bytes accessed | tf_op | source)
XLA Modules:
  0.0 85.7 jit_solution(14593589342753376547)
XLA Ops:
  0.0 84.1 %gated_ffn.1 = bf16[64,1024]{1,0:T(8,128)(2,1)} custom-call(bf16[64,1024]{1,0:T(8,128)(2,1)} %act_hbm.1, f32[8,128]{1,0:T(8,128)} %bitcast.6, bf16[3696,1024]{1,0:T(8,128)(2,1)} %bitcast.5, f32[2,1848]{1,0:T(2,128)} %gate_up_scale.1, bf16[1848,1024]{1,0:T(8,128)(2,1)} %down_hbm.1, f32[1,1024]{1,0:T(1,128)} %bitcast.7), custom_call_target="tpu_custom_call" | custom-call | tf_op jit(solution)/shard_map/gated_ffn/pallas_call | solution.py:301
  84.1 1.6 %copy.8 = bf16[64,1024]{1,0:T(8,128)(2,1)} copy(bf16[64,1024]{1,0:T(8,128)(2,1)} %gated_ffn.1) | data formatting | bytes 262144

commit v4 on v3

--- a/solution.py
+++ b/solution.py
@@ -274,19 +274,24 @@
         "A": stage_a, "B": stage_b, "C": stage_c, "D": stage_d,
         "E": stage_e, "F": stage_f, "J": stage_j,
     }
-    for words in ORDER:
-        for word in words.split():
-            name, piece, chunk = word
-            if piece == ".":
-                stages[name](int(chunk))
-            else:
-                stages[name](int(chunk), int(piece))
-    for copy in copies.values():
-        copy.wait_send()
-    for i in range(n):
-        for _, copy in to_rows(i):
-            copy.wait_send()
-    for skip, build in out_sends:
+    words = " ".join(ORDER).split()
+    early = 0
+    for at, word in enumerate(words):
+        name, piece, chunk = word
+        if at == len(words) - 1:
+            for copy in copies.values():
+                copy.wait_send()
+            for i in range(n):
+                for _, copy in to_rows(i):
+                    copy.wait_send()
+            early = len(out_sends) - 24
+            for skip, build in out_sends[:early]:
+                unless(skip, lambda build=build: build().wait_send())
+        if piece == ".":
+            stages[name](int(chunk))
+        else:
+            stages[name](int(chunk), int(piece))
+    for skip, build in out_sends[early:]:
         unless(skip, lambda build=build: build().wait_send())
 
 

time: 87.3 us -> 87 us (level)
  no operation moved by 1% of the time
where the time goes in v4:
time: 87 us; the launch traced here: 85.3 us
  Pallas kernels  83.8 us (96%)
  local copies, waits for them, and re-layouts  1.57 us (2%)
    pallas_call x1, Pallas kernels, body(): pl.pallas_call(kernel, out_shape=jax.ShapeDtypeStruct((local_rows, width)...  83.8 us

profile of v4, /device:TPU:0, one launch (start us, length us, event | category | flops | bytes accessed | tf_op | source)
XLA Modules:
  0.0 85.3 jit_solution(16042632353094074677)
XLA Ops:
  0.0 83.8 %gated_ffn.1 = bf16[64,1024]{1,0:T(8,128)(2,1)} custom-call(bf16[64,1024]{1,0:T(8,128)(2,1)} %act_hbm.1, f32[8,128]{1,0:T(8,128)} %bitcast.6, bf16[3696,1024]{1,0:T(8,128)(2,1)} %bitcast.5, f32[2,1848]{1,0:T(2,128)} %gate_up_scale.1, bf16[1848,1024]{1,0:T(8,128)(2,1)} %down_hbm.1, f32[1,1024]{1,0:T(1,128)} %bitcast.7), custom_call_target="tpu_custom_call" | custom-call | tf_op jit(solution)/shard_map/gated_ffn/pallas_call | solution.py:306
  83.8 1.6 %copy.8 = bf16[64,1024]{1,0:T(8,128)(2,1)} copy(bf16[64,1024]{1,0:T(8,128)(2,1)} %gated_ffn.1) | data formatting | bytes 262144
